TPU v7x, 128 devices: a whole 4x4x4 slice. The times are simulated.
128 devices in a mesh: dp: 16 (over z, y), tp: 8 (over x, core).
Axes of the slice: x: 4, y: 4, z: 4, core: 2. Of those that a mesh axis runs over, the one named last changes fastest.
Arguments:
- x_in: bfloat16 [3, 2, 128, 192, 768], P(None, None, 'dp')
- u_pre: bfloat16 [3, 2, 128, 192, 3072], P(None, None, 'dp', None, 'tp')
- w_up: bfloat16 [3, 768, 3072], P(None, None, 'tp')
- w_down: bfloat16 [3, 3072, 768], P(None, 'tp')
- d_out: bfloat16 [2, 128, 192, 768], P(None, 'dp')
- noise_up: float32 [3, 768, 3072], P(None, 'dp', 'tp')
- noise_down: float32 [3, 3072, 768], P(None, 'tp', 'dp')
- clip_norm: float32 [1], replicated
- noise_mult: float32 [1], replicated
Outputs:
- output 1: float32 [3, 768, 3072], P(None, 'dp', 'tp')
- output 2: float32 [3, 3072, 768], P(None, 'tp', 'dp')
- output 3: bfloat16 [2, 128, 192, 768], P(None, 'dp')
All inputs are finite; a program needn't handle non-finite values.
Results may differ from a plain program's by a relative error of at most 0.0177694.
Values are sent between devices in bfloat16 or wider.
A program may use at most 1 GiB of HBM per device.

v0:
```python
import jax
import jax.numpy as jnp
from jax import lax
from jax.sharding import PartitionSpec as P, NamedSharding


def solution(mesh):
    dp_size = mesh.shape["dp"]

    def local_pass(x_in, u_pre, w_up, w_down, d_out, noise_up, noise_down, clip_norm, noise_mult):
        n_layers = x_in.shape[0]
        examples = d_out.shape[0] * d_out.shape[1] * dp_size
        grad_cot = d_out
        norm_part = jnp.zeros(d_out.shape[:2], jnp.float32)
        saved_acts = []
        for layer_idx in reversed(range(n_layers)):
            x_layer = x_in[layer_idx]
            gelu_out, gelu_vjp = jax.vjp(jax.nn.gelu, u_pre[layer_idx].astype(jnp.float32))
            hidden = gelu_out.astype(jnp.bfloat16)
            d_act = jnp.einsum("mbtd,nd->mbtn", grad_cot, w_down[layer_idx], preferred_element_type=jnp.float32)
            d_hid = gelu_vjp(d_act)[0].astype(jnp.bfloat16)
            part_back = jnp.einsum("mbtn,dn->mbtd", d_hid, w_up[layer_idx], preferred_element_type=jnp.float32).astype(jnp.bfloat16)
            back_sum = lax.psum(part_back, "tp")
            gram_hid = jnp.einsum("mbtn,mbsn->mbts", hidden, hidden, preferred_element_type=jnp.float32)
            gram_cot = jnp.einsum("mbtd,mbsd->mbts", grad_cot, grad_cot, preferred_element_type=jnp.float32)
            gram_x = jnp.einsum("mbtd,mbsd->mbts", x_layer, x_layer, preferred_element_type=jnp.float32)
            gram_dh = jnp.einsum("mbtn,mbsn->mbts", d_hid, d_hid, preferred_element_type=jnp.float32)
            norm_part = norm_part + jnp.sum(gram_hid * gram_cot + gram_x * gram_dh, axis=(2, 3))
            saved_acts.append((layer_idx, x_layer, hidden, d_hid, grad_cot))
            grad_cot = (grad_cot.astype(jnp.float32) + back_sum.astype(jnp.float32)).astype(jnp.bfloat16)
        norm_vec = lax.psum(norm_part, "tp")
        clip_col = jnp.minimum(1.0, clip_norm[0] / jnp.sqrt(norm_vec))[:, :, None, None]
        noise_scale = noise_mult[0] * clip_norm[0]
        up_grads = [None] * n_layers
        down_grads = [None] * n_layers
        for layer_idx, x_layer, hidden, d_hid, cot_layer in saved_acts:
            scaled_dh = (d_hid * clip_col).astype(jnp.bfloat16)
            scaled_cot = (cot_layer * clip_col).astype(jnp.bfloat16)
            up_part = jnp.einsum("mbtd,mbtn->dn", x_layer, scaled_dh, preferred_element_type=jnp.float32)
            down_part = jnp.einsum("mbtn,mbtd->nd", hidden, scaled_cot, preferred_element_type=jnp.float32)
            up_sum = lax.psum_scatter(up_part, "dp", scatter_dimension=0, tiled=True)
            down_sum = lax.psum_scatter(down_part, "dp", scatter_dimension=1, tiled=True)
            up_grads[layer_idx] = (up_sum + noise_scale * noise_up[layer_idx]) / examples
            down_grads[layer_idx] = (down_sum + noise_scale * noise_down[layer_idx]) / examples
        return jnp.stack(up_grads), jnp.stack(down_grads), grad_cot

    in_specs = (P(None, None, "dp", None, None), P(None, None, "dp", None, "tp"), P(None, None, "tp"), P(None, "tp", None), P(None, "dp", None, None), P(None, "dp", "tp"), P(None, "tp", "dp"), P(), P())
    out_specs = (P(None, "dp", "tp"), P(None, "tp", "dp"), P(None, "dp", None, None))
    return jax.shard_map(local_pass, mesh=mesh, in_specs=in_specs, out_specs=out_specs, check_vma=False)
```

profile of v0, /device:TPU:0, one launch (start us, length us, event | category | flops | bytes accessed | tf_op | source)
XLA Modules:
  0.0 648.9 jit_solution(4361110819657952749)
XLA Ops:
  7.2 8.5 %fusion.17 = bf16[2,8,192,384]{3,2,1,0:T(8,128)(2,1)S(1)} fusion(bf16[2,8,192,768]{3,2,1,0:T(8,128)(2,1)} %param.13, bf16[3,2,8,192,384]{4,3,2,1,0:T(8,128)(2,1)} %param.10, bf16[3,384,768]{2,1,0:T(8,128)(2,1)} %param.12), kind=kOutput, calls=%fused_computation.38 | convolution fusion | flops 1836711936 | bytes 10027008 | tf_op jit(solution)/shard_map/mbtd,nd->mbtn/dot_general | solution.py:20
  15.7 5.3 convolution_convert_fusion.2
  21.3 7.7 %fusion.29 = (bf16[2,8,192,384]{3,2,1,0:T(8,128)(2,1)}, bf16[2,8,192,384]{3,2,1,0:T(8,128)(2,1)S(1)}, bf16[2,8,192,384]{3,2,1,0:T(8,128)(2,1)S(1)}) fusion(bf16[3,2,8,192,384]{4,3,2,1,0:T(8,128)(2,1)} %param.10), kind=kLoop, calls=%fused_computation.50 | loop fusion | flops 35389440 | bytes 14155776 | tf_op jit(solution)/shard_map/convert_element_type | solution.py:19
  29.1 1.4 copy-done.5
  30.5 2.6 fusion.116
  33.1 7.6 %fusion.110 = f32[2,8,192,192]{3,2,1,0:T(8,128)} fusion(bf16[3,2,8,192,768]{4,3,2,1,0:T(8,128)(2,1)} %param.9), kind=kOutput, calls=%fused_computation.129 | convolution fusion | flops 905969664 | bytes 7077888 | tf_op jit(solution)/shard_map/mbtd,mbsd->mbts/dot_general | solution.py:26
  40.7 1.0 fusion.112
  42.4 3.1 fusion.109
  45.6 3.1 fusion.108
  48.6 1.4 fusion.113
  50.0 0.5 copy-done.10
  50.5 1.3 add_reduce_fusion.2
  51.9 46.1 %all-reduce.12.cloned.1.call-done = bf16[2,8,192,768]{3,2,1,0:T(8,128)(2,1)} async-done(((bf16[2,8,192,768]{3,2,1,0:T(8,128)(2,1)}), bf16[2,8,192,768]{3,2,1,0:T(8,128)(2,1)}) %all-reduce.12.cloned.1.call-update) | async-done | bytes 4718608 | tf_op jit(solution)/shard_map/psum | solution.py:23
  97.9 5.2 fusion
  103.1 8.2 %fusion.14 = bf16[2,8,192,384]{3,2,1,0:T(8,128)(2,1)S(1)} fusion(bf16[2,8,192,768]{3,2,1,0:T(8,128)(2,1)S(1)} %fusion, bf16[3,2,8,192,384]{4,3,2,1,0:T(8,128)(2,1)} %param.10, bf16[3,384,768]{2,1,0:T(8,128)(2,1)} %param.12), kind=kOutput, calls=%fused_computation.35 | convolution fusion | flops 1836711936 | bytes 10027008 | tf_op jit(solution)/shard_map/mbtd,nd->mbtn/dot_general | solution.py:20
  111.4 1.4 copy-done.2
  112.8 5.5 convolution_convert_fusion.1
  118.4 3.5 fusion.114
  121.9 11.5 %slice_bitcast_fusion = (bf16[2,8,192,768]{3,2,1,0:T(8,128)(2,1)}, bf16[2,8,192,768]{3,2,1,0:T(8,128)(2,1)}, bf16[2,8,192,768]{3,2,1,0:T(8,128)(2,1)}) fusion(bf16[3,2,8,192,768]{4,3,2,1,0:T(8,128)(2,1)} %param.9), kind=kLoop, calls=%fused_computation.72 | loop fusion | bytes 28311552 | tf_op jit(solution)/shard_map/squeeze | solution.py:17
  133.5 1.4 fusion.115
  135.1 0.9 copy-done.9
  136.1 1.2 add_reduce_fusion.1
  137.3 55.4 %all-reduce.14.cloned.1.call-done = bf16[2,8,192,768]{3,2,1,0:T(8,128)(2,1)} async-done(((bf16[2,8,192,768]{3,2,1,0:T(8,128)(2,1)}), bf16[2,8,192,768]{3,2,1,0:T(8,128)(2,1)}) %all-reduce.14.cloned.1.call-update) | async-done | bytes 4718608 | tf_op jit(solution)/shard_map/psum | solution.py:23
  192.7 5.2 fusion.2
  197.9 8.2 %fusion.11 = bf16[2,8,192,384]{3,2,1,0:T(8,128)(2,1)S(1)} fusion(bf16[2,8,192,768]{3,2,1,0:T(8,128)(2,1)S(1)} %fusion.2, bf16[3,2,8,192,384]{4,3,2,1,0:T(8,128)(2,1)} %param.10, bf16[3,384,768]{2,1,0:T(8,128)(2,1)} %param.12), kind=kOutput, calls=%fused_computation.32 | convolution fusion | flops 1836711936 | bytes 10027008 | tf_op jit(solution)/shard_map/mbtd,nd->mbtn/dot_general | solution.py:20
  206.1 3.1 fusion.117
  209.2 5.4 convolution_convert_fusion
  214.6 6.5 %add_reduce_fusion = f32[2,8]{1,0:T(2,128)S(1)} fusion(f32[2,8,192,192]{3,2,1,0:T(8,128)} %fusion.110, f32[2,8,192,192]{3,2,1,0:T(8,128)} %fusion.116, f32[2,8,192,192]{3,2,1,0:T(8,128)} %fusion.117, bf16[2,8,192,384]{3,2,1,0:T(8,128)(2,1)} %copy-done.4), kind=kOutput, calls=%fused_computation.75 | convolution fusion | flops 455344128 | bytes 9437248 | tf_op jit(solution)/shard_map/mbtn,mbsn->mbts/dot_general | solution.py:27
  221.2 14.1 %psum.30 = f32[2,8]{1,0:T(2,128)S(1)} all-reduce(f32[2,8]{1,0:T(2,128)S(1)} %add_add_fusion), channel_id=1, replica_groups=mesh['dp'=16,'tp'=8] {'tp'}, use_global_device_ids=true, to_apply=%region_5.0 | all-reduce | flops 16 | bytes 128 | tf_op jit(solution)/shard_map/psum | solution.py:31
  235.8 4.6 multiply_convert_fusion.2
  240.4 5.5 fusion.54
  246.0 5.5 fusion.59
  251.5 3.1 fusion.64
  254.7 53.8 %all-reduce.16.cloned.1.call-done = bf16[2,8,192,768]{3,2,1,0:T(8,128)(2,1)} async-done(((bf16[2,8,192,768]{3,2,1,0:T(8,128)(2,1)}), bf16[2,8,192,768]{3,2,1,0:T(8,128)(2,1)}) %all-reduce.16.cloned.1.call-update) | async-done | bytes 4718608 | tf_op jit(solution)/shard_map/psum | solution.py:23
  308.5 15.0 %fusion.5 = (bf16[2,8,192,768]{3,2,1,0:T(8,128)(2,1)}, bf16[2,8,192,768]{3,2,1,0:T(8,128)(2,1)}, bf16[2,8,192,768]{3,2,1,0:T(8,128)(2,1)S(1)}, bf16[2,8,192,768]{3,2,1,0:T(8,128)(2,1)}) fusion(bf16[2,8,192,768]{3,2,1,0:T(8,128)(2,1)} %copy-done.1, bf16[2,8,192,768]{3,2,1,0:T(8,128)(2,1)} %all-reduce.16.cloned.1.call-done, ...), kind=kLoop, calls=%fused_computation.11 | loop fusion | flops 28311552 | bytes 37748800 | tf_op jit(solution)/shard_map/convert_element_type | solution.py:30
  323.5 3.7 fusion.74
  327.4 6.9 %fusion.79 = f32[384,768]{0,1:T(8,128)} fusion(bf16[2,8,192,768]{3,2,1,0:T(8,128)(2,1)} %get-tuple-element.24, bf16[2,8,192,384]{3,2,1,0:T(8,128)(2,1)} %copy-done.7), kind=kOutput, calls=%fused_computation.92 | convolution fusion | flops 1811939328 | bytes 8257536 | tf_op jit(solution)/shard_map/mbtn,mbtd->nd/dot_general | solution.py:40
  334.4 6.1 fusion.69
  341.7 0.6 dynamic-slice
  342.9 67.6 %all-reduce.18.cloned.1.call-done = (f32[768,384]{0,1:T(8,128)}, f32[768,384]{0,1:T(8,128)}, f32[768,384]{0,1:T(8,128)}) async-done(((f32[768,384]{0,1:T(8,128)}, f32[768,384]{0,1:T(8,128)}, f32[768,384]{0,1:T(8,128)}), (f32[768,384]{0,1:T(8,128)}, f32[768,384]{0,1:T(8,128)}, f32[768,384]{0,1:T(8,128)})) %all-reduce.18.cloned.1.call-update) | async-done | bytes 3538960
  410.5 1.3 fusion.97
  412.0 1.1 fusion.101
  413.2 0.7 pad_maximum_fusion
  413.9 73.0 %reduce-scatter.15.cloned.1.call-done = f32[384,48]{0,1:T(8,128)} async-done(((f32[384,768]{0,1:T(8,128)}), f32[384,48]{0,1:T(8,128)}) %reduce-scatter.15.cloned.1.call-update) | async-done | bytes 73744
  486.9 76.6 %reduce-scatter.17.cloned.1.call-done = f32[384,48]{0,1:T(8,128)} async-done(((f32[384,768]{0,1:T(8,128)}), f32[384,48]{0,1:T(8,128)}) %reduce-scatter.17.cloned.1.call-update) | async-done | bytes 73744
  563.5 76.7 %reduce-scatter.13.cloned.1.call-done = f32[384,48]{0,1:T(8,128)} async-done(((f32[384,768]{0,1:T(8,128)}), f32[384,48]{0,1:T(8,128)}) %reduce-scatter.13.cloned.1.call-update) | async-done | bytes 73744
  640.2 1.0 fusion.107
  641.2 0.7 pad_maximum_fusion.1
  (71 shorter events, 2.2 us)
Async XLA Ops:
  7.2 90.8 %all-reduce.12.cloned.1.call-start = ((), (), s32[]{:S(2)}) async-start(), calls=%async_computation.3 | async-start | bytes 9437184 | tf_op jit(solution)/shard_map/psum | solution.py:23
  21.1 171.6 %all-reduce.14.cloned.1.call-start = ((), (), s32[]{:S(2)}) async-start(), calls=%async_computation.4 | async-start | bytes 9437184 | tf_op jit(solution)/shard_map/psum | solution.py:23
  29.1 1.4 copy-start.5
  29.1 11.7 %copy-start.7 = (bf16[2,8,192,384]{3,2,1,0:T(8,128)(2,1)}, bf16[2,8,192,384]{3,2,1,0:T(8,128)(2,1)S(1)}, u32[]{:S(2)}) copy-start(bf16[2,8,192,384]{3,2,1,0:T(8,128)(2,1)S(1)} %get-tuple-element.13) | copy-start | bytes 7077892
  30.5 11.9 %slice-start.4 = ((s8[14155776]{0:T(1024)(128)(4,1)}), s8[4194304]{0:T(1024)(128)(4,1)S(1)}, s32[]{:S(2)}) async-start(s8[14155776]{0:T(1024)(128)(4,1)} %bitcast.169), calls=%async_computation.14 | async-start | bytes 8388608
  30.5 11.9 %slice-start.5 = ((s8[14155776]{0:T(1024)(128)(4,1)}), s8[4194304]{0:T(1024)(128)(4,1)S(1)}, s32[]{:S(2)}) async-start(s8[14155776]{0:T(1024)(128)(4,1)} %bitcast.169), calls=%async_computation.15 | async-start | bytes 8388608
  33.1 9.3 %slice-start.6 = ((s8[14155776]{0:T(1024)(128)(4,1)}), s8[4194304]{0:T(1024)(128)(4,1)S(1)}, s32[]{:S(2)}) async-start(s8[14155776]{0:T(1024)(128)(4,1)} %bitcast.169), calls=%async_computation.16 | async-start | bytes 8388608
  40.7 1.7 slice-start.7
  42.4 6.2 slice-start.2
  45.6 3.1 slice-start.3
  48.6 1.9 copy-start.10
  103.1 8.2 %copy-start = (bf16[2,8,192,768]{3,2,1,0:T(8,128)(2,1)}, bf16[2,8,192,768]{3,2,1,0:T(8,128)(2,1)S(1)}, u32[]{:S(2)}) copy-start(bf16[2,8,192,768]{3,2,1,0:T(8,128)(2,1)S(1)} %fusion) | copy-start | bytes 14155780
  111.3 1.4 copy-start.2
  118.3 190.1 %all-reduce.16.cloned.1.call-start = ((), (), s32[]{:S(2)}) async-start(), calls=%async_computation.5 | async-start | bytes 9437184 | tf_op jit(solution)/shard_map/psum | solution.py:23
  118.4 15.1 %slice-start = ((s8[4718592]{0:T(1024)(128)(4,1)}), s8[4194304]{0:T(1024)(128)(4,1)S(1)}, s32[]{:S(2)}) async-start(s8[4718592]{0:T(1024)(128)(4,1)} %bitcast.165), calls=%async_computation.10 | async-start | bytes 8388608
  121.9 11.5 %slice-start.1 = ((s8[4718592]{0:T(1024)(128)(4,1)}), s8[524288]{0:T(1024)(128)(4,1)S(1)}, s32[]{:S(2)}) async-start(s8[4718592]{0:T(1024)(128)(4,1)} %bitcast.165), calls=%async_computation.11 | async-start | bytes 1048576
  133.5 1.7 copy-start.3
  133.5 2.6 copy-start.9
  197.9 8.2 %copy-start.1 = (bf16[2,8,192,768]{3,2,1,0:T(8,128)(2,1)}, bf16[2,8,192,768]{3,2,1,0:T(8,128)(2,1)S(1)}, u32[]{:S(2)}) copy-start(bf16[2,8,192,768]{3,2,1,0:T(8,128)(2,1)S(1)} %fusion.2) | copy-start | bytes 14155780
  206.1 3.1 copy-start.4
  235.3 175.2 %all-reduce.18.cloned.1.call-start = ((), (), s32[]{:S(2)}) async-start(), calls=%async_computation.9 | async-start | bytes 7077888
  240.4 11.1 %slice-start.8 = ((s8[4718592]{0:T(1024)(128)(4,1)}), s8[4194304]{0:T(1024)(128)(4,1)S(1)}, s32[]{:S(2)}) async-start(s8[4718592]{0:T(1024)(128)(4,1)} %bitcast.171), calls=%async_computation.18 | async-start | bytes 8388608
  246.0 5.5 slice-start.9
  254.6 68.9 %copy-start.8 = (bf16[2,8,192,384]{3,2,1,0:T(8,128)(2,1)S(1)}, bf16[2,8,192,384]{3,2,1,0:T(8,128)(2,1)}, u32[]{:S(2)}) copy-start(bf16[2,8,192,384]{3,2,1,0:T(8,128)(2,1)} %get-tuple-element.12) | copy-start | bytes 7077892
  254.6 232.2 %reduce-scatter.15.cloned.1.call-start = ((), (), s32[]{:S(2)}) async-start(), calls=%async_computation.7 | async-start | bytes 1253376
  327.2 236.3 %reduce-scatter.17.cloned.1.call-start = ((), (), s32[]{:S(2)}) async-start(), calls=%async_computation.8 | async-start | bytes 1253376
  327.4 7.0 %copy-start.6 = (bf16[2,8,192,384]{3,2,1,0:T(8,128)(2,1)S(1)}, bf16[2,8,192,384]{3,2,1,0:T(8,128)(2,1)}, u32[]{:S(2)}) copy-start(bf16[2,8,192,384]{3,2,1,0:T(8,128)(2,1)} %copy-done.5) | copy-start | bytes 7077892
  334.3 305.8 %reduce-scatter.13.cloned.1.call-start = ((), (), s32[]{:S(2)}) async-start(), calls=%async_computation.6 | async-start | bytes 1253376
  334.4 6.8 %copy-start.11 = (f32[3,48,384]{2,1,0:T(8,128)S(1)}, f32[3,48,384]{2,1,0:T(8,128)}, u32[]{:S(2)}) copy-start(f32[3,48,384]{2,1,0:T(8,128)} %param.14) | copy-start | bytes 663556
  334.4 7.2 %copy-start.13 = (u32[128]{0:T(128)S(1)}, u32[128]{0:T(128)}, u32[]{:S(2)}) copy-start(u32[128]{0:T(128)} %constant.31) | copy-start | bytes 1540
  340.5 299.7 %copy-start.12 = (f32[3,384,48]{1,2,0:T(8,128)S(1)}, f32[3,384,48]{1,2,0:T(8,128)}, u32[]{:S(2)}) copy-start(f32[3,384,48]{1,2,0:T(8,128)} %param.15) | copy-start | bytes 663556
Sparse Core Ops, SparseCore 0:
  21.2 76.6 all-reduce.11
  118.5 74.2 all-reduce.13
  235.4 73.0 all-reduce.15
  312.1 98.2 all-reduce.17
  413.5 73.3 reduce-scatter.14
  489.9 73.4 reduce-scatter.16
  566.7 73.4 reduce-scatter.12
where the time goes:
time: 655 us; the launch traced here: 649 us
  waiting for transfers between devices  449 us (69%)
  matrix products  108 us (16%)
  other arithmetic  42.6 us (7%)
  local copies, waits for them, and re-layouts  17.4 us (3%)
  between operations  16.7 us (3%)
  blocking collectives  14.1 us (2%)
    unnamed x11, waiting for transfers between devices  294 us
    psum x3, waiting for transfers between devices, local_pass(): back_sum = lax.psum(part_back, 'tp')  155 us
    convert_element_type x3, other arithmetic, local_pass(): (grad_cot.astype(jnp.float32) + back_sum.astype(jnp.float32)).astype(jnp....  25.4 us
    dot_general x3, matrix products, local_pass(): jnp.einsum('mbtd,nd->mbtn', grad_cot, w_down[layer_idx], preferred_elemen...  24.9 us
    dot_general x3, matrix products, local_pass(): jnp.einsum('mbtn,mbtd->nd', hidden, scaled_cot, preferred_element_type=jn...  16.6 us
    dot_general x3, matrix products, local_pass(): jnp.einsum('mbtn,dn->mbtd', d_hid, w_up[layer_idx], preferred_element_typ...  16.3 us
    dot_general x3, matrix products, local_pass(): jnp.einsum('mbtd,mbtn->dn', x_layer, scaled_dh, preferred_element_type=jn...  14.2 us
    psum x1, blocking collectives, local_pass(): norm_vec = lax.psum(norm_part, 'tp')  14.1 us
  transfers between devices with their start and end apart: 7, of which 7 were waited for; matrix products, arithmetic and copies ran while one was open for 15% of the time, Pallas kernels for 0%

commit v1 on v0

v1 whole, which is shorter than its diff:
```python
import math

import jax
import jax.numpy as jnp
from jax import lax
from jax.experimental import pallas as pl
from jax.experimental.pallas import tpu as pltpu
from jax.sharding import PartitionSpec as P

MESH = pl.DeviceIdType.MESH
F32, BF16 = jnp.float32, jnp.bfloat16
N_CHUNK = 4
RING = 4
K_TANH = math.sqrt(2.0 / math.pi)
(D2D, S1L, S1R, SDL, SDR, S2L, S2R, A1L, A1R, A2L, A2R, FO, FR, FL, FA, FB) = range(16)
N_ROLE = 16
NT = (((1,), (1,)), ((), ()))
TN = (((0,), (0,)), ((), ()))


def step_kernel(x_hbm, u_hbm, w1_hbm, w2_hbm, do_hbm, nu_ref, nd_ref, clip_ref, mult_ref,
                gu_ref, gd_ref, din_hbm,
                u_s, dh_s, dz_s, w1_s, w2_s, xs, da_s, p_s, rd2d, r1, rdir, r2, g_s, q1, q2,
                nrm, nsend, nrecv, clip_s,
                ssem, rsem, gsem_s, gsem_r, nsem_s, nsem_r, usem, wsem, dsem, xsem, osem):
    n_layers, n_chunk, rows, hid = u_s.shape
    dim = dz_s.shape[-1]
    n_ex, _, seq = nrm.shape
    ex_per = n_ex // n_chunk
    piece = rows // 16
    n_item = n_layers * n_chunk
    dp, tp = lax.axis_index("dp"), lax.axis_index("tp")
    xi, core = tp // 2, tp % 2
    zi, yi = dp // RING, dp % RING

    def up(i, by=1):
        return (i + by) % RING

    x_l, x_r, x_o = up(xi, 3), up(xi, 1), up(xi, 2)
    partner = (dp, xi * 2 + 1 - core)
    dev_l, dev_r, dev_o = (dp, x_l * 2 + core), (dp, x_r * 2 + core), (dp, x_o * 2 + core)
    dev_yl, dev_yr = (zi * RING + up(yi, 3), tp), (zi * RING + up(yi), tp)
    dev_zl, dev_zr = (up(zi, 3) * RING + yi, tp), (up(zi) * RING + yi, tp)

    def remote(src, dst, send, recv, dev):
        return pltpu.make_async_remote_copy(src_ref=src, dst_ref=dst, send_sem=send, recv_sem=recv,
                                            device_id=dev, device_id_type=MESH)

    def load_u(layer, c):
        return pltpu.make_async_copy(u_hbm.at[layer, c], u_s.at[layer, c], usem.at[layer, c])

    def load_w(which, layer):
        src, dst = ((w1_hbm, w1_s), (w2_hbm, w2_s))[which]
        return pltpu.make_async_copy(src.at[layer], dst.at[layer], wsem.at[which, layer])

    def load_d(c):
        return pltpu.make_async_copy(do_hbm.at[c], dz_s.at[0, c], dsem.at[c])

    def load_x(item):
        layer, c, slot = n_layers - 1 - item // n_chunk, item % n_chunk, item % 2
        return pltpu.make_async_copy(x_hbm.at[layer, c], xs.at[slot], xsem.at[slot])

    top = n_layers - 1
    load_w(1, top).start()
    load_d(0).start()
    load_u(top, 0).start()
    load_w(0, top).start()
    load_x(0).start()
    for c in range(1, n_chunk):
        load_d(c).start()
        load_u(top, c).start()
    for layer in reversed(range(top)):
        load_w(1, layer).start()
        load_w(0, layer).start()
        for c in range(n_chunk):
            load_u(layer, c).start()

    barrier = pltpu.get_barrier_semaphore()
    peers = (partner, dev_l, dev_r, dev_o, dev_yl, dev_yr, dev_zl, dev_zr)
    for dev in peers:
        pl.semaphore_signal(barrier, inc=1, device_id=dev, device_id_type=MESH)
    pl.semaphore_wait(barrier, len(peers))

    nrm[...] = jnp.zeros_like(nrm)

    def at(cc, xx, half=0, n=1):
        return pl.ds(pl.multiple_of(cc * (rows // 2) + xx * (rows // 8) + half * piece, 16), n * piece)

    def tp_copy(role, item):
        li, c, slot = item // n_chunk, item % n_chunk, item % 2
        part, znew = p_s.at[slot], dz_s.at[li + 1, c]
        send, recv = ssem.at[role, c], rsem.at[role, c]
        if role == D2D:
            half = pl.ds(pl.multiple_of((1 - core) * (rows // 2), 16), rows // 2)
            return remote(part.at[half], rd2d.at[c], send, recv, partner)
        if role in (S1L, S1R):
            h = 0 if role == S1L else 1
            return remote(part.at[at(core, x_o, h)], r1.at[c, h], send, recv, (dev_l, dev_r)[h])
        if role == SDL:
            return remote(part.at[at(core, x_l, 1)], rdir.at[c, 0], send, recv, dev_l)
        if role == SDR:
            return remote(part.at[at(core, x_r, 0)], rdir.at[c, 1], send, recv, dev_r)
        if role == S2L:
            return remote(part.at[at(core, x_l, 0)], r2.at[c, 0], send, recv, dev_l)
        if role == S2R:
            return remote(part.at[at(core, x_r, 1)], r2.at[c, 1], send, recv, dev_r)
        where, dev = {
            A1L: (at(core, xi, 0, 2), dev_l),
            A1R: (at(core, xi, 0, 2), dev_r),
            A2L: (at(core, x_r, 0), dev_l),
            A2R: (at(core, x_l, 1), dev_r),
            FO: (at(core, xi, 0, 2), partner),
            FR: (at(core, x_r, 0, 2), partner),
            FL: (at(core, x_l, 0, 2), partner),
            FA: (at(core, x_o, 0), partner),
            FB: (at(core, x_o, 1), partner),
        }[role]
        return remote(znew.at[where], znew.at[where], send, recv, dev)

    def start(item, *roles):
        for role in roles:
            tp_copy(role, item).start()

    def arrived(item, *roles):
        for role in roles:
            tp_copy(role, item).wait_recv()

    def sent(item, *roles):
        for role in roles:
            tp_copy(role, item).wait_send()

    def pair_sum(item):
        c, slot = item % n_chunk, item % 2
        arrived(item, D2D)
        base = core * (rows // 2)
        blk = rows // 8

        def add(b, _):
            mine = pl.ds(pl.multiple_of(base + b * blk, 16), blk)
            theirs = pl.ds(pl.multiple_of(b * blk, 16), blk)
            p_s[slot, mine, :] = (p_s[slot, mine, :].astype(F32) + rd2d[c, theirs, :].astype(F32)).astype(BF16)
            return 0

        lax.fori_loop(0, 4, add, 0)
        start(item, S1L, S1R, SDL, SDR)

    def relay_sum(item):
        c, slot = item % n_chunk, item % 2
        for h, come, go, xx in ((0, S1L, S2L, x_l), (1, S1R, S2R, x_r)):
            arrived(item, come)
            where = at(core, xx, h)
            p_s[slot, where, :] = (p_s[slot, where, :].astype(F32) + r1[c, h].astype(F32)).astype(BF16)
            start(item, go)

    def own_sum(item):
        li, c, slot = item // n_chunk, item % n_chunk, item % 2
        for h, far, near in ((0, S2L, SDR), (1, S2R, SDL)):
            arrived(item, near, far)
            where = at(core, xi, h)
            total = p_s[slot, where, :].astype(F32) + r2[c, h].astype(F32) + rdir[c, 1 - h].astype(F32)
            dz_s[li + 1, c, where, :] = (dz_s[li, c, where, :].astype(F32) + total).astype(BF16)
        start(item, A1L, A1R, FO)

    def gather_relay(item):
        arrived(item, A1L)
        start(item, A2L, FR)
        arrived(item, A1R)
        start(item, A2R, FL)
        sent(item, D2D, S1L, S1R, SDL, SDR, S2L, S2R)

    def gather_cross(item):
        arrived(item, A2L)
        start(item, FA)
        arrived(item, A2R)
        start(item, FB)

    def out_copy(c):
        return pltpu.make_async_copy(dz_s.at[n_layers, c], din_hbm.at[c], osem.at[c])

    def gather_end(item):
        arrived(item, FO, FR, FL, FA, FB)
        sent(item, A1L, A1R, A2L, A2R, FO, FR, FL, FA, FB)

        @pl.when(item >= n_item - n_chunk)
        def _():
            out_copy(item % n_chunk).start()

    def compute_dh(item):
        li, c = item // n_chunk, item % n_chunk
        layer = top - li

        @pl.when(c == 0)
        def _():
            load_w(1, layer).wait()
            load_w(0, layer).wait()

        @pl.when(li == 0)
        def _():
            load_d(c).wait()

        load_u(layer, c).wait()
        da_s[...] = lax.dot_general(dz_s[li, c], w2_s[layer], NT, preferred_element_type=F32)
        blk = 32

        def act(b, _):
            r = pl.ds(pl.multiple_of(b * blk, blk), blk)
            u = u_s[layer, c, r, :].astype(F32)
            u2 = u * u
            th = jnp.tanh(K_TANH * (u + 0.044715 * (u2 * u)))
            cdf = 0.5 * (1.0 + th)
            slope = cdf + (0.5 * u) * (1.0 - th * th) * K_TANH * (1.0 + (3 * 0.044715) * u2)
            u_s[layer, c, r, :] = (u * cdf).astype(BF16)
            dh_s[layer, c, r, :] = (slope * da_s[r, :]).astype(BF16)
            return 0

        lax.fori_loop(0, rows // blk, act, 0)

    def compute_back(item):
        li, c, slot = item // n_chunk, item % n_chunk, item % 2
        layer = top - li
        for part in range(2):
            cc = 1 - core if part == 0 else core
            r = pl.ds(pl.multiple_of(cc * (rows // 2), 16), rows // 2)
            p_s[slot, r, :] = lax.dot_general(dh_s[layer, c, r, :], w1_s[layer], NT,
                                              preferred_element_type=F32).astype(BF16)
            if part == 0:
                start(item, D2D)

    def compute_norm(item):
        li, c = item // n_chunk, item % n_chunk
        layer = top - li
        load_x(item).wait()

        def one(e, _):
            r = pl.ds(pl.multiple_of(e * seq, 16), seq)

            def gram(v):
                return lax.dot_general(v, v, NT, preferred_element_type=F32)

            total = (gram(u_s[layer, c, r, :]) * gram(dz_s[li, c, r, :])
                     + gram(xs[item % 2, r, :]) * gram(dh_s[layer, c, r, :]))
            nrm[c * ex_per + e] += jnp.sum(total.reshape(seq // 8, 8, seq), axis=0)
            return 0

        lax.fori_loop(0, ex_per, one, 0)

    def slot_body(t, _):
        live = t < n_item
        one_back = jnp.logical_and(t >= 1, t - 1 < n_item)
        two_back = t >= 2

        @pl.when(t + 1 < n_item)
        def _():
            load_x(t + 1).start()

        @pl.when(one_back)
        def _():
            pair_sum(t - 1)

        @pl.when(two_back)
        def _():
            gather_relay(t - 2)

        @pl.when(live)
        def _():
            compute_dh(t)

        @pl.when(one_back)
        def _():
            relay_sum(t - 1)

        @pl.when(two_back)
        def _():
            gather_cross(t - 2)

        @pl.when(live)
        def _():
            compute_back(t)

        @pl.when(one_back)
        def _():
            own_sum(t - 1)

        @pl.when(live)
        def _():
            compute_norm(t)

        @pl.when(two_back)
        def _():
            gather_end(t - 2)

        return 0

    lax.fori_loop(0, n_item + 2, slot_body, 0)

    load_x(0).start()
    local = jnp.sum(jnp.sum(nrm[...], axis=1), axis=-1, keepdims=True)
    nsend[0] = jnp.broadcast_to(local, nsend.shape[1:])
    first = remote(nsend.at[0], nrecv.at[0], nsem_s.at[0], nsem_r.at[0], partner)
    first.start()
    first.wait_recv()
    nsend[1] = nsend[0] + nrecv[0]
    rest = [remote(nsend.at[1], nrecv.at[i + 1], nsem_s.at[i + 1], nsem_r.at[i + 1], dev)
            for i, dev in enumerate((dev_l, dev_r, dev_o))]
    for cp in rest:
        cp.start()
    for cp in rest:
        cp.wait_recv()
    norm = nsend[1] + nrecv[1] + nrecv[2] + nrecv[3]
    factor = jnp.minimum(1.0, clip_ref[0] / jnp.sqrt(norm))
    for e in range(n_ex):
        clip_s[e] = jnp.broadcast_to(factor[e:e + 1, :], clip_s.shape[1:])
    first.wait_send()
    for cp in rest:
        cp.wait_send()

    def grad_view(k, kind, phase, j, h):
        if phase == 0:
            n = RING // 2
            if kind == 0:
                return g_s.at[k, pl.ds(h * n, n), j]
            return g_s.at[k, j, pl.ds(h * n, n)]
        n = g_s.shape[3] // 2
        if kind == 0:
            return g_s.at[k, j, yi, pl.ds(h * n, n)]
        return g_s.at[k, zi, j, pl.ds(h * n, n)]

    def ring_of(kind, phase):
        if (kind == 0) == (phase == 0):
            return yi, dev_yl, dev_yr
        return zi, dev_zl, dev_zr

    def grad_copy(k, kind, phase, role):
        me, d_l, d_r = ring_of(kind, phase)
        buf = (q1, q2)[phase]
        j, h = ((up(me, 2), 0), (up(me, 2), 1), (up(me, 3), 1), (up(me, 1), 0), (up(me, 3), 0), (up(me, 1), 1))[role]
        return remote(grad_view(k, kind, phase, j, h), buf.at[k, role], gsem_s.at[phase, role, k],
                      gsem_r.at[phase, role, k], d_r if role % 2 else d_l)

    def ring_start(p, kind, phase):
        k = 2 * p + kind
        for role in range(4):
            grad_copy(k, kind, phase, role).start()

    def ring_relay(p, kind, phase):
        k = 2 * p + kind
        me, _, _ = ring_of(kind, phase)
        buf = (q1, q2)[phase]
        for h in range(2):
            grad_copy(k, kind, phase, h).wait_recv()
            view = grad_view(k, kind, phase, up(me, 1 if h else 3), h)
            view[...] = view[...] + buf[k, h]
            grad_copy(k, kind, phase, 4 + h).start()

    def ring_end(p, kind, phase):
        k = 2 * p + kind
        me, _, _ = ring_of(kind, phase)
        buf = (q1, q2)[phase]
        for h in range(2):
            grad_copy(k, kind, phase, 3 - h).wait_recv()
            grad_copy(k, kind, phase, 4 + h).wait_recv()
            view = grad_view(k, kind, phase, me, h)
            view[...] = view[...] + buf[k, 3 - h] + buf[k, 4 + h]

    def ring_sent(p, kind, phase):
        for role in range(6):
            grad_copy(2 * p + kind, kind, phase, role).wait_send()

    inv = 1.0 / (n_ex * RING * RING)
    scale = mult_ref[0] * clip_ref[0]

    def finish(p, kind):
        k, layer = 2 * p + kind, top - p
        out, noise = ((gu_ref, nu_ref), (gd_ref, nd_ref))[kind]
        out[layer] = (g_s[k, zi, yi] + scale * noise[layer]) * inv

    def weight_grad(p, kind):
        k, layer = 2 * p + kind, top - p

        def one(c, _):
            if kind == 0:
                item = p * n_chunk + c

                @pl.when(item + 1 < n_item)
                def _():
                    load_x(item + 1).start()

                load_x(item).wait()
            for e in range(ex_per):
                f = clip_s[c * ex_per + e][0:1, 0:1]
                r = pl.ds(e * seq, seq)
                if kind == 0:
                    dh_s[layer, c, r, :] = (dh_s[layer, c, r, :].astype(F32) * f).astype(BF16)
                else:
                    dz_s[p, c, r, :] = (dz_s[p, c, r, :].astype(F32) * f).astype(BF16)
            if kind == 0:
                add = lax.dot_general(xs[c % 2], dh_s[layer, c], TN, preferred_element_type=F32)
            else:
                add = lax.dot_general(dz_s[p, c], u_s[layer, c], TN, preferred_element_type=F32)
            add = add.reshape(g_s.shape[1:])

            @pl.when(c == 0)
            def _():
                g_s[k] = add

            @pl.when(c > 0)
            def _():
                g_s[k] += add

            return 0

        lax.fori_loop(0, n_chunk, one, 0)

    def pair_body(p, _):
        def back(n):
            return jnp.logical_and(p >= n, p - n < n_layers)

        @pl.when(back(0))
        def _():
            weight_grad(p, 0)
            ring_start(p, 0, 0)

        @pl.when(back(1))
        def _():
            ring_relay(p - 1, 1, 0)

        @pl.when(back(0))
        def _():
            weight_grad(p, 1)
            ring_start(p, 1, 0)
            ring_relay(p, 0, 0)

        @pl.when(back(2))
        def _():
            ring_relay(p - 2, 0, 1)
            ring_relay(p - 2, 1, 1)

        @pl.when(back(1))
        def _():
            ring_end(p - 1, 0, 0)
            ring_start(p - 1, 0, 1)
            ring_end(p - 1, 1, 0)
            ring_start(p - 1, 1, 1)

        @pl.when(back(2))
        def _():
            for kind in range(2):
                ring_end(p - 2, kind, 1)
                finish(p - 2, kind)
                ring_sent(p - 2, kind, 0)
                ring_sent(p - 2, kind, 1)

        return 0

    lax.fori_loop(0, n_layers + 2, pair_body, 0)
    for c in range(n_chunk):
        out_copy(c).wait()


def solution(mesh):
    n_dp, n_tp = mesh.shape["dp"], mesh.shape["tp"]

    def local(x_in, u_pre, w_up, w_down, d_out, noise_up, noise_down, clip_norm, noise_mult):
        n_layers, micro, batch, seq, dim = x_in.shape
        hid = u_pre.shape[-1]
        n_ex = micro * batch
        rows = n_ex * seq // N_CHUNK
        piece, grad_rows = rows // 16, dim // n_dp
        x4 = x_in.reshape(n_layers, N_CHUNK, rows, dim)
        u4 = u_pre.reshape(n_layers, N_CHUNK, rows, hid)
        d4 = d_out.reshape(N_CHUNK, rows, dim)
        anyspace = pl.BlockSpec(memory_space=pl.ANY)
        vmem = pl.BlockSpec(memory_space=pltpu.VMEM)
        smem = pl.BlockSpec(memory_space=pltpu.SMEM)
        dma = pltpu.SemaphoreType.DMA
        tokens = n_ex * seq
        flops = 2 * n_layers * tokens * hid * dim * 4 + 4 * n_layers * tokens * seq * (hid + dim)
        g_up, g_down, d_in = pl.pallas_call(
            step_kernel,
            out_shape=(
                jax.ShapeDtypeStruct((n_layers, grad_rows, hid), F32),
                jax.ShapeDtypeStruct((n_layers, grad_rows, hid), F32),
                jax.ShapeDtypeStruct((N_CHUNK, rows, dim), BF16),
            ),
            in_specs=[anyspace] * 5 + [vmem, vmem, smem, smem],
            out_specs=(vmem, vmem, anyspace),
            scratch_shapes=[
                pltpu.VMEM((n_layers, N_CHUNK, rows, hid), BF16),
                pltpu.VMEM((n_layers, N_CHUNK, rows, hid), BF16),
                pltpu.VMEM((n_layers + 1, N_CHUNK, rows, dim), BF16),
                pltpu.VMEM((n_layers, dim, hid), BF16),
                pltpu.VMEM((n_layers, hid, dim), BF16),
                pltpu.VMEM((2, rows, dim), BF16),
                pltpu.VMEM((rows, hid), F32),
                pltpu.VMEM((2, rows, dim), BF16),
                pltpu.VMEM((N_CHUNK, rows // 2, dim), BF16),
                pltpu.VMEM((N_CHUNK, 2, piece, dim), BF16),
                pltpu.VMEM((N_CHUNK, 2, piece, dim), BF16),
                pltpu.VMEM((N_CHUNK, 2, piece, dim), BF16),
                pltpu.VMEM((2 * n_layers, RING, RING, grad_rows, hid), F32),
                pltpu.VMEM((2 * n_layers, 6, RING // 2, grad_rows, hid), F32),
                pltpu.VMEM((2 * n_layers, 6, grad_rows // 2, hid), F32),
                pltpu.VMEM((n_ex, 8, seq), F32),
                pltpu.VMEM((2, n_ex, 128), F32),
                pltpu.VMEM((4, n_ex, 128), F32),
                pltpu.VMEM((n_ex, 8, 128), F32),
                dma((N_ROLE, N_CHUNK)),
                dma((N_ROLE, N_CHUNK)),
                dma((2, 6, 2 * n_layers)),
                dma((2, 6, 2 * n_layers)),
                dma((4,)),
                dma((4,)),
                dma((n_layers, N_CHUNK)),
                dma((2, n_layers)),
                dma((N_CHUNK,)),
                dma((2,)),
                dma((N_CHUNK,)),
            ],
            compiler_params=pltpu.CompilerParams(
                collective_id=0, has_side_effects=True, vmem_limit_bytes=67_043_328
            ),
            cost_estimate=pl.CostEstimate(flops=flops, bytes_accessed=50_000_000, transcendentals=n_layers * tokens * hid),
            name="clipped_step",
        )(x4, u4, w_up, w_down, d4, noise_up, jnp.transpose(noise_down, (0, 2, 1)), clip_norm, noise_mult)
        return g_up, jnp.transpose(g_down, (0, 2, 1)), d_in.reshape(d_out.shape)

    in_specs = (P(None, None, "dp", None, None), P(None, None, "dp", None, "tp"), P(None, None, "tp"),
                P(None, "tp", None), P(None, "dp", None, None), P(None, "dp", "tp"), P(None, "tp", "dp"), P(), P())
    out_specs = (P(None, "dp", "tp"), P(None, "tp", "dp"), P(None, "dp", None, None))
    return jax.shard_map(local, mesh=mesh, in_specs=in_specs, out_specs=out_specs, check_vma=False)
```

time: 655 us -> 245 us (0.37)
  waiting for transfers between devices: 449 us -> 0 us
  Pallas kernels: 0 us -> 235 us
  matrix products: 108 us -> 0 us
  other arithmetic: 42.6 us -> 0 us
  between operations: 16.7 us -> 1.93 us
  blocking collectives: 14.1 us -> 0 us
  local copies, waits for them, and re-layouts: 17.4 us -> 8.21 us
    unnamed x11 -> x0, waiting for transfers between devices: 294 us -> none
    pallas_call x0 -> x1, Pallas kernels: none -> 235 us  [local(): pl.pallas_call(step_kernel, out_shape=(jax.ShapeDtypeStruct((n_layers, gr...]
    psum x3 -> x0, waiting for transfers between devices: 155 us -> none  [local_pass(): back_sum = lax.psum(part_back, 'tp')]
    dot_general x24 -> x0, matrix products: 108 us -> none  [the longest x3 24.9 us: local_pass(): jnp.einsum('mbtd,nd->mbtn', grad_cot, w_down[layer_idx], preferred_elemen...]
    convert_element_type x5 -> x0, other arithmetic: 37.7 us -> none  [the longest x3 25.4 us: local_pass(): (grad_cot.astype(jnp.float32) + back_sum.astype(jnp.float32)).astype(jnp....]
    psum x1 -> x0, blocking collectives: 14.1 us -> none  [local_pass(): norm_vec = lax.psum(norm_part, 'tp')]
    squeeze x1 -> x0, local copies, waits for them, and re-layouts: 11.5 us -> none  [local_pass(): x_layer = x_in[layer_idx]]
  transfers between devices with their start and end apart: 7 -> 0, of which waited for: 7 -> 0; matrix products, arithmetic and copies ran while one was open for 15% -> 0% of each run, Pallas kernels for 0% -> 0%
where the time goes in v1:
time: 245 us
  Pallas kernels  235 us (96%)
  local copies, waits for them, and re-layouts  8.21 us (3%)
    pallas_call x1, Pallas kernels, local(): pl.pallas_call(step_kernel, out_shape=(jax.ShapeDtypeStruct((n_layers, gr...  235 us
    unnamed x3, local copies, waits for them, and re-layouts  8.21 us

profile of v1, /device:TPU:0, one launch (start us, length us, event | category | flops | bytes accessed | tf_op | source)
XLA Modules:
  0.0 244.7 jit_solution(13261620067682386064)
XLA Ops:
  1.9 234.5 %clipped_step.1 = (f32[3,48,384]{2,1,0:T(8,128)}, f32[3,48,384]{2,1,0:T(8,128)}, bf16[4,768,768]{2,1,0:T(8,128)(2,1)}) custom-call(bf16[3,4,768,768]{3,2,1,0:T(8,128)(2,1)} %bitcast.8, bf16[3,4,768,384]{3,2,1,0:T(8,128)(2,1)} %bitcast.9, bf16[3,768,384]{2,1,0:T(8,128)(2,1)} %w1_hbm.1, bf16[3,384,768]{2,1,0:T(8,128)(2,1)} %w2_hbm.1, ...), custom_call_target="tpu_custom_call" | custom-call | flops 29896998912 | bytes 50000000 | tf_op jit(solution)/shard_map/clipped_step/pallas_call | solution.py:478
  236.5 1.6 copy.17
  238.1 1.6 copy.18
  239.7 4.9 %copy.19 = bf16[2,8,192,768]{3,2,1,0:T(8,128)(2,1)} copy(bf16[2,8,192,768]{3,2,1,0:T(8,128)(2,1)} %bitcast.6) | data formatting | bytes 9437184

commit v2 on v1

--- a/solution.py
+++ b/solution.py
@@ -18,11 +18,11 @@
 TN = (((0,), (0,)), ((), ()))
 
 
-def step_kernel(x_hbm, u_hbm, w1_hbm, w2_hbm, do_hbm, nu_ref, nd_ref, clip_ref, mult_ref,
+def step_kernel(x_hbm, u_hbm, w1_hbm, w2_hbm, do_hbm, clip_hbm,
                 gu_ref, gd_ref, din_hbm,
                 u_s, dh_s, dz_s, w1_s, w2_s, xs, da_s, p_s, rd2d, r1, rdir, r2, g_s, q1, q2,
-                nrm, nsend, nrecv, clip_s,
-                ssem, rsem, gsem_s, gsem_r, nsem_s, nsem_r, usem, wsem, dsem, xsem, osem):
+                nrm, nsend, nrecv, clip_s, clip_ref,
+                ssem, rsem, gsem_s, gsem_r, nsem_s, nsem_r, usem, wsem, dsem, xsem, osem, csem):
     n_layers, n_chunk, rows, hid = u_s.shape
     dim = dz_s.shape[-1]
     n_ex, _, seq = nrm.shape
@@ -60,6 +60,7 @@
         layer, c, slot = n_layers - 1 - item // n_chunk, item % n_chunk, item % 2
         return pltpu.make_async_copy(x_hbm.at[layer, c], xs.at[slot], xsem.at[slot])
 
+    load_c = pltpu.make_async_copy(clip_hbm, clip_ref, csem)
     top = n_layers - 1
     load_w(1, top).start()
     load_d(0).start()
@@ -74,20 +75,19 @@
         load_w(0, layer).start()
         for c in range(n_chunk):
             load_u(layer, c).start()
+    load_c.start()
 
     barrier = pltpu.get_barrier_semaphore()
     peers = (partner, dev_l, dev_r, dev_o, dev_yl, dev_yr, dev_zl, dev_zr)
     for dev in peers:
         pl.semaphore_signal(barrier, inc=1, device_id=dev, device_id_type=MESH)
-    pl.semaphore_wait(barrier, len(peers))
-
-    nrm[...] = jnp.zeros_like(nrm)
+
 
     def at(cc, xx, half=0, n=1):
         return pl.ds(pl.multiple_of(cc * (rows // 2) + xx * (rows // 8) + half * piece, 16), n * piece)
 
     def tp_copy(role, item):
-        li, c, slot = item // n_chunk, item % n_chunk, item % 2
+        li, c, slot = item // n_chunk, item % n_chunk, item % n_chunk
         part, znew = p_s.at[slot], dz_s.at[li + 1, c]
         send, recv = ssem.at[role, c], rsem.at[role, c]
         if role == D2D:
@@ -130,7 +130,7 @@
             tp_copy(role, item).wait_send()
 
     def pair_sum(item):
-        c, slot = item % n_chunk, item % 2
+        c, slot = item % n_chunk, item % n_chunk
         arrived(item, D2D)
         base = core * (rows // 2)
         blk = rows // 8
@@ -142,10 +142,10 @@
             return 0
 
         lax.fori_loop(0, 4, add, 0)
-        start(item, S1L, S1R, SDL, SDR)
+        start(item, S1L, S1R)
 
     def relay_sum(item):
-        c, slot = item % n_chunk, item % 2
+        c, slot = item % n_chunk, item % n_chunk
         for h, come, go, xx in ((0, S1L, S2L, x_l), (1, S1R, S2R, x_r)):
             arrived(item, come)
             where = at(core, xx, h)
@@ -153,7 +153,7 @@
             start(item, go)
 
     def own_sum(item):
-        li, c, slot = item // n_chunk, item % n_chunk, item % 2
+        li, c, slot = item // n_chunk, item % n_chunk, item % n_chunk
         for h, far, near in ((0, S2L, SDR), (1, S2R, SDL)):
             arrived(item, near, far)
             where = at(core, xi, h)
@@ -216,7 +216,7 @@
         lax.fori_loop(0, rows // blk, act, 0)
 
     def compute_back(item):
-        li, c, slot = item // n_chunk, item % n_chunk, item % 2
+        li, c, slot = item // n_chunk, item % n_chunk, item % n_chunk
         layer = top - li
         for part in range(2):
             cc = 1 - core if part == 0 else core
@@ -244,75 +244,27 @@
 
         lax.fori_loop(0, ex_per, one, 0)
 
-    def slot_body(t, _):
-        live = t < n_item
-        one_back = jnp.logical_and(t >= 1, t - 1 < n_item)
-        two_back = t >= 2
-
-        @pl.when(t + 1 < n_item)
-        def _():
-            load_x(t + 1).start()
-
-        @pl.when(one_back)
-        def _():
-            pair_sum(t - 1)
-
-        @pl.when(two_back)
-        def _():
-            gather_relay(t - 2)
-
-        @pl.when(live)
-        def _():
-            compute_dh(t)
-
-        @pl.when(one_back)
-        def _():
-            relay_sum(t - 1)
-
-        @pl.when(two_back)
-        def _():
-            gather_cross(t - 2)
-
-        @pl.when(live)
-        def _():
-            compute_back(t)
-
-        @pl.when(one_back)
-        def _():
-            own_sum(t - 1)
-
-        @pl.when(live)
-        def _():
-            compute_norm(t)
-
-        @pl.when(two_back)
-        def _():
-            gather_end(t - 2)
-
-        return 0
-
-    lax.fori_loop(0, n_item + 2, slot_body, 0)
-
-    load_x(0).start()
-    local = jnp.sum(jnp.sum(nrm[...], axis=1), axis=-1, keepdims=True)
-    nsend[0] = jnp.broadcast_to(local, nsend.shape[1:])
-    first = remote(nsend.at[0], nrecv.at[0], nsem_s.at[0], nsem_r.at[0], partner)
-    first.start()
-    first.wait_recv()
-    nsend[1] = nsend[0] + nrecv[0]
-    rest = [remote(nsend.at[1], nrecv.at[i + 1], nsem_s.at[i + 1], nsem_r.at[i + 1], dev)
-            for i, dev in enumerate((dev_l, dev_r, dev_o))]
-    for cp in rest:
-        cp.start()
-    for cp in rest:
-        cp.wait_recv()
-    norm = nsend[1] + nrecv[1] + nrecv[2] + nrecv[3]
-    factor = jnp.minimum(1.0, clip_ref[0] / jnp.sqrt(norm))
-    for e in range(n_ex):
-        clip_s[e] = jnp.broadcast_to(factor[e:e + 1, :], clip_s.shape[1:])
-    first.wait_send()
-    for cp in rest:
-        cp.wait_send()
+    def clip_factors():
+        load_c.wait()
+        local = jnp.sum(jnp.sum(nrm[...], axis=1), axis=-1, keepdims=True)
+        nsend[0] = jnp.broadcast_to(local, nsend.shape[1:])
+        first = remote(nsend.at[0], nrecv.at[0], nsem_s.at[0], nsem_r.at[0], partner)
+        first.start()
+        first.wait_recv()
+        nsend[1] = nsend[0] + nrecv[0]
+        rest = [remote(nsend.at[1], nrecv.at[i + 1], nsem_s.at[i + 1], nsem_r.at[i + 1], dev)
+                for i, dev in enumerate((dev_l, dev_r, dev_o))]
+        for cp in rest:
+            cp.start()
+        for cp in rest:
+            cp.wait_recv()
+        norm = nsend[1] + nrecv[1] + nrecv[2] + nrecv[3]
+        factor = jnp.minimum(1.0, clip_ref[0] / jnp.sqrt(norm))
+        for e in range(n_ex):
+            clip_s[e] = jnp.broadcast_to(factor[e:e + 1, :], clip_s.shape[1:])
+        first.wait_send()
+        for cp in rest:
+            cp.wait_send()
 
     def grad_view(k, kind, phase, j, h):
         if phase == 0:
@@ -366,13 +318,8 @@
         for role in range(6):
             grad_copy(2 * p + kind, kind, phase, role).wait_send()
 
-    inv = 1.0 / (n_ex * RING * RING)
-    scale = mult_ref[0] * clip_ref[0]
-
     def finish(p, kind):
-        k, layer = 2 * p + kind, top - p
-        out, noise = ((gu_ref, nu_ref), (gd_ref, nd_ref))[kind]
-        out[layer] = (g_s[k, zi, yi] + scale * noise[layer]) * inv
+        (gu_ref, gd_ref)[kind][top - p] = g_s[2 * p + kind, zi, yi]
 
     def weight_grad(p, kind):
         k, layer = 2 * p + kind, top - p
@@ -392,11 +339,11 @@
                 if kind == 0:
                     dh_s[layer, c, r, :] = (dh_s[layer, c, r, :].astype(F32) * f).astype(BF16)
                 else:
-                    dz_s[p, c, r, :] = (dz_s[p, c, r, :].astype(F32) * f).astype(BF16)
+                    xs[1, r, :] = (dz_s[p, c, r, :].astype(F32) * f).astype(BF16)
             if kind == 0:
                 add = lax.dot_general(xs[c % 2], dh_s[layer, c], TN, preferred_element_type=F32)
             else:
-                add = lax.dot_general(dz_s[p, c], u_s[layer, c], TN, preferred_element_type=F32)
+                add = lax.dot_general(xs[1], u_s[layer, c], TN, preferred_element_type=F32)
             add = add.reshape(g_s.shape[1:])
 
             @pl.when(c == 0)
@@ -411,48 +358,109 @@
 
         lax.fori_loop(0, n_chunk, one, 0)
 
-    def pair_body(p, _):
-        def back(n):
-            return jnp.logical_and(p >= n, p - n < n_layers)
-
-        @pl.when(back(0))
+    late = n_item - n_chunk
+
+    def slot_body(t, _):
+        i_s = t - 1 - 2 * (t // (late + 3))
+        i_a = t - 2 - 2 * (t // (late + 4))
+        i_e = t - 3 - 2 * (t // (late + 5))
+
+        def span(lo, n):
+            return jnp.logical_and(t >= lo, t < lo + n)
+
+        on_s = jnp.logical_or(span(1, late), span(late + 3, n_chunk))
+        on_a = jnp.logical_or(span(2, late), span(late + 4, n_chunk))
+        on_e = jnp.logical_or(span(3, late), span(late + 5, n_chunk))
+        live = t < n_item
+        p = t - n_item
+
+        @pl.when(live)
+        def _():
+            load_x((t + 1) % n_item).start()
+
+        @pl.when(on_s)
+        def _():
+            pair_sum(i_s)
+
+        @pl.when(on_a)
+        def _():
+            own_sum(i_a)
+
+        @pl.when(on_s)
+        def _():
+            start(i_s, SDL, SDR)
+
+        @pl.when(jnp.logical_and(live, t > 0))
+        def _():
+            compute_dh(t)
+
+        @pl.when(t == n_item)
+        def _():
+            clip_factors()
+
+        @pl.when(span(n_item, n_layers))
         def _():
             weight_grad(p, 0)
             ring_start(p, 0, 0)
 
-        @pl.when(back(1))
+        @pl.when(on_e)
+        def _():
+            gather_cross(i_e)
+
+        @pl.when(live)
+        def _():
+            compute_back(t)
+
+        @pl.when(span(n_item + 1, n_layers))
         def _():
             ring_relay(p - 1, 1, 0)
 
-        @pl.when(back(0))
+        @pl.when(on_s)
+        def _():
+            relay_sum(i_s)
+
+        @pl.when(live)
+        def _():
+            compute_norm(t)
+
+        @pl.when(span(n_item, n_layers))
         def _():
             weight_grad(p, 1)
             ring_start(p, 1, 0)
             ring_relay(p, 0, 0)
 
-        @pl.when(back(2))
+        @pl.when(on_a)
+        def _():
+            gather_relay(i_a)
+
+        @pl.when(span(n_item + 2, n_layers))
         def _():
             ring_relay(p - 2, 0, 1)
             ring_relay(p - 2, 1, 1)
 
-        @pl.when(back(1))
+        @pl.when(span(n_item + 1, n_layers))
         def _():
             ring_end(p - 1, 0, 0)
             ring_start(p - 1, 0, 1)
             ring_end(p - 1, 1, 0)
             ring_start(p - 1, 1, 1)
 
-        @pl.when(back(2))
-        def _():
-            for kind in range(2):
-                ring_end(p - 2, kind, 1)
-                finish(p - 2, kind)
-                ring_sent(p - 2, kind, 0)
-                ring_sent(p - 2, kind, 1)
+        @pl.when(on_e)
+        def _():
+            gather_end(i_e)
 
         return 0
 
-    lax.fori_loop(0, n_layers + 2, pair_body, 0)
+    nrm[...] = jnp.zeros_like(nrm)
+    compute_dh(0)
+    pl.semaphore_wait(barrier, len(peers))
+    lax.fori_loop(0, n_item + n_layers + 2, slot_body, 0)
+    for p in range(n_layers):
+        for kind in range(2):
+            ring_end(p, kind, 1)
+            finish(p, kind)
+            ring_sent(p, kind, 0)
+            ring_sent(p, kind, 1)
     for c in range(n_chunk):
         out_copy(c).wait()
 
@@ -471,7 +479,6 @@
         d4 = d_out.reshape(N_CHUNK, rows, dim)
         anyspace = pl.BlockSpec(memory_space=pl.ANY)
         vmem = pl.BlockSpec(memory_space=pltpu.VMEM)
-        smem = pl.BlockSpec(memory_space=pltpu.SMEM)
         dma = pltpu.SemaphoreType.DMA
         tokens = n_ex * seq
         flops = 2 * n_layers * tokens * hid * dim * 4 + 4 * n_layers * tokens * seq * (hid + dim)
@@ -482,7 +489,7 @@
                 jax.ShapeDtypeStruct((n_layers, grad_rows, hid), F32),
                 jax.ShapeDtypeStruct((N_CHUNK, rows, dim), BF16),
             ),
-            in_specs=[anyspace] * 5 + [vmem, vmem, smem, smem],
+            in_specs=[anyspace] * 6,
             out_specs=(vmem, vmem, anyspace),
             scratch_shapes=[
                 pltpu.VMEM((n_layers, N_CHUNK, rows, hid), BF16),
@@ -492,7 +499,7 @@
                 pltpu.VMEM((n_layers, hid, dim), BF16),
                 pltpu.VMEM((2, rows, dim), BF16),
                 pltpu.VMEM((rows, hid), F32),
-                pltpu.VMEM((2, rows, dim), BF16),
+                pltpu.VMEM((N_CHUNK, rows, dim), BF16),
                 pltpu.VMEM((N_CHUNK, rows // 2, dim), BF16),
                 pltpu.VMEM((N_CHUNK, 2, piece, dim), BF16),
                 pltpu.VMEM((N_CHUNK, 2, piece, dim), BF16),
@@ -504,6 +511,7 @@
                 pltpu.VMEM((2, n_ex, 128), F32),
                 pltpu.VMEM((4, n_ex, 128), F32),
                 pltpu.VMEM((n_ex, 8, 128), F32),
+                pltpu.SMEM((1,), F32),
                 dma((N_ROLE, N_CHUNK)),
                 dma((N_ROLE, N_CHUNK)),
                 dma((2, 6, 2 * n_layers)),
@@ -515,14 +523,19 @@
                 dma((N_CHUNK,)),
                 dma((2,)),
                 dma((N_CHUNK,)),
+                dma,
             ],
             compiler_params=pltpu.CompilerParams(
                 collective_id=0, has_side_effects=True, vmem_limit_bytes=67_043_328
             ),
             cost_estimate=pl.CostEstimate(flops=flops, bytes_accessed=50_000_000, transcendentals=n_layers * tokens * hid),
             name="clipped_step",
-        )(x4, u4, w_up, w_down, d4, noise_up, jnp.transpose(noise_down, (0, 2, 1)), clip_norm, noise_mult)
-        return g_up, jnp.transpose(g_down, (0, 2, 1)), d_in.reshape(d_out.shape)
+        )(x4, u4, w_up, w_down, d4, clip_norm)
+        inv = 1.0 / (n_ex * n_dp)
+        scale = noise_mult[0] * clip_norm[0]
+        g_up = (g_up + scale * noise_up) * inv
+        g_down = (jnp.transpose(g_down, (0, 2, 1)) + scale * noise_down) * inv
+        return g_up, g_down, d_in.reshape(d_out.shape)
 
     in_specs = (P(None, None, "dp", None, None), P(None, None, "dp", None, "tp"), P(None, None, "tp"),
                 P(None, "tp", None), P(None, "dp", None, None), P(None, "dp", "tp"), P(None, "tp", "dp"), P(), P())

time: 245 us -> 179 us (0.73)
  Pallas kernels: 235 us -> 168 us
  other arithmetic: 0 us -> 3.51 us
  local copies, waits for them, and re-layouts: 8.21 us -> 4.94 us
    pallas_call x1, Pallas kernels: 235 us -> 168 us  [local(): pl.pallas_call(step_kernel, out_shape=(jax.ShapeDtypeStruct((n_layers, gr...]
    mul x0 -> x2, other arithmetic: none -> 3.51 us  [the longest x1 1.76 us: local(): g_up = (g_up + scale * noise_up) * inv]
    unnamed x3 -> x1, local copies, waits for them, and re-layouts: 8.21 us -> 4.94 us
where the time goes in v2:
time: 179 us; the launch traced here: 178 us
  Pallas kernels  168 us (94%)
  local copies, waits for them, and re-layouts  4.94 us (3%)
  other arithmetic  3.51 us (2%)
  between operations  1.93 us (1%)
    pallas_call x1, Pallas kernels, local(): pl.pallas_call(step_kernel, out_shape=(jax.ShapeDtypeStruct((n_layers, gr...  168 us
    unnamed x1, local copies, waits for them, and re-layouts  4.94 us

profile of v2, /device:TPU:0, one launch (start us, length us, event | category | flops | bytes accessed | tf_op | source)
XLA Modules:
  0.0 178.4 jit_solution(14613815192445111366)
XLA Ops:
  1.9 168.0 %clipped_step.1 = (f32[3,48,384]{2,1,0:T(8,128)}, f32[3,48,384]{2,1,0:T(8,128)}, bf16[4,768,768]{2,1,0:T(8,128)(2,1)}) custom-call(bf16[3,4,768,768]{3,2,1,0:T(8,128)(2,1)} %bitcast.10, bf16[3,4,768,384]{3,2,1,0:T(8,128)(2,1)} %bitcast.11, bf16[3,768,384]{2,1,0:T(8,128)(2,1)} %w1_hbm.1, bf16[3,384,768]{2,1,0:T(8,128)(2,1)} %w2_hbm.1, ...), custom_call_target="tpu_custom_call" | custom-call | flops 29896998912 | bytes 50000000 | tf_op jit(solution)/shard_map/clipped_step/pallas_call | solution.py:485
  169.9 1.8 add_multiply_fusion
  171.7 1.8 fusion
  173.4 4.9 %copy.15 = bf16[2,8,192,768]{3,2,1,0:T(8,128)(2,1)} copy(bf16[2,8,192,768]{3,2,1,0:T(8,128)(2,1)} %bitcast.9) | data formatting | bytes 9437184
